TPU v7x, 32 devices: a whole 2x2x4 slice. The times are simulated.
32 devices in a mesh: pb: 2 (over x), col: 16 (over z, y, core).
Axes of the slice: x: 2, y: 2, z: 4, core: 2. Of those that a mesh axis runs over, the one named last changes fastest.
Arguments:
- queries: bfloat16 [4096, 1024], P(('pb', 'col')), may hold values from -64 to 64
- candidates: bfloat16 [16384, 1024], P(('col', 'pb')), may hold values from -5 to 5
- grades: int32 [4096, 16384], P('pb', 'col'), may hold values from 0 to 4
- query_weights: float32 [4096], P('pb'), may hold values from -0.046875 to 0.046875
Outputs:
- losses: float32 [4096], P('pb')
- query_grad: bfloat16 [4096, 1024], P(('pb', 'col'))
- cand_grad: bfloat16 [16384, 1024], P(('col', 'pb'))
All inputs are finite; a program needn't handle non-finite values.
Results may differ from a plain program's by a relative error of at most 0.0071.
Values may be sent and summed in bfloat16 or wider, within the bound.
A program may use at most 128 MiB of HBM per device.

v0:
```python
import math
import jax
import jax.numpy as jnp
from jax import lax
from jax.sharding import PartitionSpec as P

GRADES = 5
lowest = -1e30


def combined_all(x, axis, combine):
    everything = jax.tree.map(lambda part: lax.all_gather(part, axis), x)
    leading = jax.tree.map(lambda part: part[0], everything)

    def step(k, so_far):
        return combine(so_far, jax.tree.map(lambda part: part[k], everything))

    return lax.fori_loop(1, lax.axis_size(axis), step, leading)


def grade_levels(maxima, masses, counts):
    levels = []
    running = maxima[0]
    seen_count = counts[0] * 0.0
    for bucket in range(maxima.shape[0]):
        running = jnp.maximum(running, maxima[bucket])
        seen_count = seen_count + counts[bucket]
        summed = masses[0] * jnp.exp(maxima[0] - running)
        for lesser in range(1, bucket + 1):
            summed = summed + masses[lesser] * jnp.exp(maxima[lesser] - running)
        present = seen_count > 0.0
        levels.append(
            jnp.where(present, running + jnp.log(jnp.where(present, summed, 1.0)), running)
        )
    return levels


def slope_factors(maxima, levels, counts):
    factors = []
    for bucket in range(maxima.shape[0]):
        summed = counts[bucket] * jnp.exp(maxima[bucket] - levels[bucket])
        for higher in range(bucket + 1, maxima.shape[0]):
            summed = summed + counts[higher] * jnp.exp(maxima[bucket] - levels[higher])
        factors.append(summed)
    return factors


def local(queries, candidates, grades, query_weights):
    width = queries.shape[1]
    scaling = 1.0 / math.sqrt(width)
    cand_block = lax.all_gather(candidates, "pb", axis=0, tiled=True)
    query_block = lax.all_gather(queries, "col", axis=0, tiled=True)
    scores = jnp.dot(query_block, cand_block.T, preferred_element_type=jnp.float32) * scaling
    members = [grades == bucket for bucket in range(GRADES)]
    totals_local = jnp.sum(scores, axis=1)
    counts_local = jnp.stack([jnp.sum(member.astype(jnp.float32), axis=1) for member in members])
    maxima_local = jnp.stack(
        [jnp.max(jnp.where(member, scores, lowest), axis=1) for member in members]
    )

    def spread_rows(values):
        picked = jnp.zeros(scores.shape, jnp.float32)
        for bucket in range(GRADES):
            picked = jnp.where(members[bucket], values[bucket][:, None], picked)
        return picked

    def masses_from(expo):
        return jnp.stack(
            [jnp.sum(jnp.where(members[bucket], expo, 0.0), axis=1) for bucket in range(GRADES)]
        )

    def combine(former, latter):
        merged = jnp.maximum(former[0], latter[0])
        rescaled = former[1] * jnp.exp(former[0] - merged) + latter[1] * jnp.exp(latter[0] - merged)
        return (merged, rescaled, former[2] + latter[2], former[3] + latter[3])

    expo = jnp.exp(scores - spread_rows(maxima_local))
    maxima, masses, counts, totals = combined_all(
        (maxima_local, masses_from(expo), counts_local, totals_local), "col", combine
    )
    columns_all = grades.shape[1] * lax.axis_size("col")
    levels = grade_levels(maxima, masses, counts)
    weighted = counts[0] * levels[0]
    for bucket in range(1, GRADES):
        weighted = weighted + counts[bucket] * levels[bucket]
    losses = (weighted - totals) / columns_all
    factors = jnp.stack(slope_factors(maxima, levels, counts))
    scaled_factors = factors * jnp.exp(maxima_local - maxima)
    slopes = (query_weights[:, None] * (spread_rows(scaled_factors) * expo - 1.0)).astype(
        jnp.bfloat16
    )
    query_grad = lax.psum_scatter(
        jnp.dot(slopes, cand_block, preferred_element_type=jnp.float32) * scaling,
        "col",
        scatter_dimension=0,
        tiled=True,
    ).astype(jnp.bfloat16)
    cand_grad = lax.psum_scatter(
        lax.dot_general(
            slopes, query_block, (((0,), (0,)), ((), ())), preferred_element_type=jnp.float32
        )
        * scaling,
        "pb",
        scatter_dimension=0,
        tiled=True,
    )
    return (losses, query_grad, cand_grad.astype(jnp.bfloat16))


def solution(mesh):
    in_specs = (P(("pb", "col"), None), P(("col", "pb"), None), P("pb", "col"), P("pb"))
    out_specs = (P("pb"), P(("pb", "col"), None), P(("col", "pb"), None))
    return jax.shard_map(local, mesh=mesh, in_specs=in_specs, out_specs=out_specs, check_vma=False)
```

profile of v0, /device:TPU:0, one launch (start us, length us, event | category | flops | bytes accessed | tf_op | source)
XLA Modules:
  0.0 426.9 jit_solution(16694783811220427614)
XLA Ops:
  7.2 0.0 all-gather.12.cloned.1.call-start
  7.2 0.7 all-gather.12.cloned.1.call-update
  7.9 0.0 all-gather.10.cloned.1.call-start
  7.9 0.7 all-gather.10.cloned.1.call-update
  8.6 0.0 reduce-scatter.5.cloned.1.call-start
  8.7 9.1 %copy.14 = s32[2048,1024]{0,1:T(8,128)} copy(s32[2048,1024]{1,0:T(8,128)} %param.8) | data formatting | bytes 16777216 | tf_op args[2]
  17.8 27.5 %all-gather.12.cloned.1.call-done = bf16[1024,1024]{1,0:T(8,128)(2,1)} async-done(((bf16[512,1024]{1,0:T(8,128)(2,1)}), bf16[1024,1024]{1,0:T(8,128)(2,1)}) %all-gather.12.cloned.1.call-update) | async-done | bytes 2097168 | tf_op jit(solution)/shard_map/all_gather | solution.py:51
  45.4 52.6 %all-gather.10.cloned.1.call-done = bf16[2048,1024]{1,0:T(8,128)(2,1)} async-done(((bf16[128,1024]{1,0:T(8,128)(2,1)}), bf16[2048,1024]{1,0:T(8,128)(2,1)}) %all-gather.10.cloned.1.call-update) | async-done | bytes 4194320 | tf_op jit(solution)/shard_map/all_gather | solution.py:52
  97.9 19.5 %multiply_reduce_fusion = (f32[2048]{0:T(1024)S(1)}, f32[2048]{0:T(1024)S(1)}, f32[2048]{0:T(1024)S(1)}, f32[2048]{0:T(1024)S(1)}, f32[2048]{0:T(1024)S(1)}, /*i...) fusion(s32[2048,1024]{0,1:T(8,128)} %copy.14, ...), kind=kOutput, calls=%fused_computation.24 | convolution fusion | flops 4334798848 | bytes 33611776 | tf_op jit(solution)/shard_map/dot_general | solution.py:53
  117.5 0.0 copy-start.5
  117.5 0.0 copy-start.6
  117.5 19.3 %all-gather.3 = f32[32768]{0:T(1024)S(1)} all-gather(f32[2048]{0:T(1024)S(1)} %get-tuple-element.236), channel_id=5, replica_groups=mesh['pb'=2,'col'=16] {'col'}, dimensions={0}, use_global_device_ids=true | all-gather | bytes 139264 | tf_op jit(solution)/shard_map/all_gather | solution.py:12
  136.8 16.7 %select_reduce_fusion = (f32[2048]{0:T(1024)S(1)}, f32[2048]{0:T(1024)S(1)}, f32[2048]{0:T(1024)S(1)}, f32[2048]{0:T(1024)S(1)}, f32[2048]{0:T(1024)}, /*index=5...) fusion(pred[2048,1024]{0,1:T(8,128)(4,1)} %get-tuple-element.282, ...), kind=kLoop, calls=%fused_computation.13 | loop fusion | flops 52410368 | bytes 27377664 | tf_op jit(solution)/shard_map/reduce_sum | solution.py:69
  153.5 0.0 copy-done.3
  153.5 0.0 copy-done.4
  153.5 0.0 copy-done.5
  153.5 0.0 copy-done.6
  153.5 0.1 stack.79
  153.6 20.8 %all-gather.6 = f32[16,5,2048]{2,1,0:T(8,128)S(1)} all-gather(f32[1,5,2048]{2,1,0:T(8,128)S(1)} %bitcast.71), channel_id=4, replica_groups=mesh['pb'=2,'col'=16] {'col'}, dimensions={0}, use_global_device_ids=true | all-gather | bytes 696320 | tf_op jit(solution)/shard_map/all_gather | solution.py:12
  174.4 0.8 stack.73
  175.2 25.6 %all-gather.5 = f32[16,5,2048]{2,1,0:T(8,128)S(1)} all-gather(f32[1,5,2048]{2,1,0:T(8,128)S(1)} %bitcast.72), channel_id=3, replica_groups=mesh['pb'=2,'col'=16] {'col'}, dimensions={0}, use_global_device_ids=true | all-gather | bytes 696320 | tf_op jit(solution)/shard_map/all_gather | solution.py:12
  200.8 1.1 copy-done.1
  201.8 0.8 stack.67
  202.6 20.7 %all-gather.4 = f32[16,5,2048]{2,1,0:T(8,128)S(1)} all-gather(f32[1,5,2048]{2,1,0:T(8,128)S(1)} %bitcast.70), channel_id=2, replica_groups=mesh['pb'=2,'col'=16] {'col'}, dimensions={0}, use_global_device_ids=true | all-gather | bytes 696320 | tf_op jit(solution)/shard_map/all_gather | solution.py:12
  223.3 1.0 copy-done.2
  224.3 15.0 %while.21 = (s32[]{:T(128)}, f32[5,2048]{1,0:T(8,128)S(1)}, f32[5,2048]{1,0:T(8,128)S(1)}, f32[5,2048]{1,0:T(8,128)S(1)}, f32[2048]{0:T(1024)S(1)}, /*index=5*/f...) while((s32[]{:T(128)}, f32[5,2048]{1,0:T(8,128)S(1)}, ...), condition=%wide.region_17.18_spmd, body=%wide.region_16.17_spmd.sunk | while | flops 73733 | bytes 409767 | solution.py:18
  224.3 0.9 fusion.46
  225.3 0.9 fusion.46
  226.3 0.9 fusion.46
  227.3 0.9 fusion.46
  228.3 0.9 fusion.46
  229.3 0.9 fusion.46
  230.3 0.9 fusion.46
  231.3 0.9 fusion.46
  232.3 0.9 fusion.46
  233.3 0.9 fusion.46
  234.3 0.9 fusion.46
  235.3 0.9 fusion.46
  236.3 0.9 fusion.46
  237.3 0.9 fusion.46
  238.3 0.9 fusion.46
  239.3 0.2 exponential_multiply_fusion.1
  239.5 0.2 multiply_add_fusion.2
  239.7 0.1 multiply_add_fusion.3
  239.8 0.1 multiply_add_fusion.4
  239.9 0.2 multiply_add_fusion.5
  240.1 0.1 stack.80
  240.2 0.0 copy-start.7
  240.2 8.7 %multiply_convert_fusion = bf16[2048,1024]{0,1:T(8,128)(2,1)S(1)} fusion(f32[2048,1024]{0,1:T(8,128)} %get-tuple-element.280, pred[2048,1024]{0,1:T(8,128)(4,1)} %get-tuple-element.282, pred[2048,1024]{0,1:T(8,128)(4,1)} %get-tuple-element.283, pred[2048,1024]{0,1:T(8,128)(4,1)} %get-tuple-element.284, pred[2048,1024]{0,1:T(8,128)(4,1)} %get-tuple-element.285, ...), kind=kLoop, calls=%fused_computation.7 | loop fusion | flops 18874368 | bytes 23117824 | tf_op jit(solution)/shard_map/convert_element_type | solution.py:89
  249.0 0.0 copy-start
  249.0 2.0 copy-done
  250.9 0.0 copy-done.7
  250.9 6.0 %convolution_multiply_fusion.1 = f32[1024,1024]{1,0:T(8,128)} fusion(bf16[2048,1024]{0,1:T(8,128)(2,1)S(1)} %multiply_convert_fusion, bf16[2048,1024]{1,0:T(8,128)(2,1)S(1)} %copy-done.7), kind=kOutput, calls=%fused_computation.31 | convolution fusion | flops 4296015872 | bytes 12582912 | tf_op jit(solution)/shard_map/dot_general | solution.py:99
  257.0 0.0 reduce-scatter.5.cloned.1.call-update
  257.0 0.0 reduce-scatter.3.cloned.1.call-start
  257.0 0.0 copy-done.8
  257.0 9.0 %convolution_multiply_fusion = f32[2048,1024]{0,1:T(8,128)} fusion(bf16[2048,1024]{0,1:T(8,128)(2,1)} %copy-done, bf16[1024,1024]{1,0:T(8,128)(2,1)S(1)} %copy-done.8), kind=kOutput, calls=%fused_computation.25 | convolution fusion | flops 4297064448 | bytes 14680064 | tf_op jit(solution)/shard_map/dot_general | solution.py:93
  266.0 0.0 reduce-scatter.3.cloned.1.call-update
  266.1 0.7 fusion.9
  266.7 44.2 %reduce-scatter.5.cloned.1.call-done = f32[512,1024]{1,0:T(8,128)} async-done(((f32[1024,1024]{1,0:T(8,128)}), f32[512,1024]{1,0:T(8,128)}) %reduce-scatter.5.cloned.1.call-update) | async-done | bytes 2097168 | tf_op jit(solution)/shard_map/reduce_scatter | solution.py:98
  310.9 2.7 convert_element_type.31
  313.7 104.8 %reduce-scatter.3.cloned.1.call-done = f32[128,1024]{0,1:T(8,128)} async-done(((f32[2048,1024]{0,1:T(8,128)}), f32[128,1024]{0,1:T(8,128)}) %reduce-scatter.3.cloned.1.call-update) | async-done | bytes 524304 | tf_op jit(solution)/shard_map/reduce_scatter | solution.py:92
  418.5 1.1 convert_element_type.30
  419.5 0.8 copy.20
  (42 shorter events, 0.4 us)
Async XLA Ops:
  7.2 38.2 %all-gather.12.cloned.1.call-start = ((), (), s32[]{:S(2)}) async-start(), calls=%async_computation.3 | async-start | bytes 3145728 | tf_op jit(solution)/shard_map/all_gather | solution.py:51
  7.9 90.0 %all-gather.10.cloned.1.call-start = ((), (), s32[]{:S(2)}) async-start(), calls=%async_computation.2 | async-start | bytes 4456448 | tf_op jit(solution)/shard_map/all_gather | solution.py:52
  8.6 302.3 %reduce-scatter.5.cloned.1.call-start = ((), (), s32[]{:S(2)}) async-start(), calls=%async_computation.5 | async-start | bytes 6291456 | tf_op jit(solution)/shard_map/reduce_scatter | solution.py:98
  117.5 36.0 %copy-start.3 = (f32[2048]{0:T(1024)}, f32[2048]{0:T(1024)S(1)}, u32[]{:S(2)}) copy-start(f32[2048]{0:T(1024)S(1)} %get-tuple-element.238) | copy-start | bytes 24580
  117.5 36.0 %copy-start.4 = (f32[2048]{0:T(1024)}, f32[2048]{0:T(1024)S(1)}, u32[]{:S(2)}) copy-start(f32[2048]{0:T(1024)S(1)} %get-tuple-element.239) | copy-start | bytes 24580
  117.5 36.0 %copy-start.5 = (f32[2048]{0:T(1024)}, f32[2048]{0:T(1024)S(1)}, u32[]{:S(2)}) copy-start(f32[2048]{0:T(1024)S(1)} %get-tuple-element.240) | copy-start | bytes 24580
  117.5 36.0 %copy-start.6 = (f32[2048]{0:T(1024)}, f32[2048]{0:T(1024)S(1)}, u32[]{:S(2)}) copy-start(f32[2048]{0:T(1024)S(1)} %get-tuple-element.241) | copy-start | bytes 24580
  200.8 1.1 copy-start.1
  223.3 1.0 copy-start.2
  240.2 10.7 %copy-start.7 = (bf16[2048,1024]{1,0:T(8,128)(2,1)S(1)}, bf16[2048,1024]{1,0:T(8,128)(2,1)}, u32[]{:S(2)}) copy-start(bf16[2048,1024]{1,0:T(8,128)(2,1)} %all-gather.10.cloned.1.call-done) | copy-start | bytes 12582916
  249.0 2.0 copy-start
  250.9 6.1 %copy-start.8 = (bf16[1024,1024]{1,0:T(8,128)(2,1)S(1)}, bf16[1024,1024]{1,0:T(8,128)(2,1)}, u32[]{:S(2)}) copy-start(bf16[1024,1024]{1,0:T(8,128)(2,1)} %all-gather.12.cloned.1.call-done) | copy-start | bytes 6291460
  257.0 161.5 %reduce-scatter.3.cloned.1.call-start = ((), (), s32[]{:S(2)}) async-start(), calls=%async_computation.4 | async-start | bytes 8912896 | tf_op jit(solution)/shard_map/reduce_scatter | solution.py:92
Sparse Core Ops, SparseCore 0:
  9.5 35.8 all-gather.11
  47.5 50.3 all-gather.9
  257.1 53.7 reduce-scatter.4
  314.9 103.5 reduce-scatter.2
where the time goes:
time: 428 us; the launch traced here: 427 us
  waiting for transfers between devices  231 us (54%)
  blocking collectives  86.4 us (20%)
  other arithmetic  44.8 us (10%)
  matrix products  34.6 us (8%)
  local copies, waits for them, and re-layouts  16 us (4%)
  between operations  13.9 us (3%)
    reduce_scatter x1, waiting for transfers between devices, local(): lax.psum_scatter(jnp.dot(slopes, cand_block, preferred_element_type=jnp.f...  105 us
    all_gather x4, blocking collectives, combined_all(): everything = jax.tree.map(lambda part: lax.all_gather(part, axis), x)  86.4 us
    all_gather x1, waiting for transfers between devices, local(): query_block = lax.all_gather(queries, 'col', axis=0, tiled=True)  52.6 us
    reduce_scatter x1, waiting for transfers between devices, local(): lax.psum_scatter(lax.dot_general(slopes, query_block, (((0,), (0,)), ((),...  44.2 us
    all_gather x1, waiting for transfers between devices, local(): cand_block = lax.all_gather(candidates, 'pb', axis=0, tiled=True)  27.5 us
    dot_general x1, matrix products, local(): jnp.dot(query_block, cand_block.T, preferred_element_type=jnp.float32)  19.5 us
    reduce_sum x1, other arithmetic, masses_from(): jnp.sum(jnp.where(members[bucket], expo, 0.0), axis=1)  16.7 us
    add x15, other arithmetic, combine(): former[1] * jnp.exp(former[0] - merged)  14.2 us
  transfers between devices with their start and end apart: 4, of which 4 were waited for; matrix products, arithmetic and copies ran while one was open for 5% of the time, Pallas kernels for 0%

commit v1 on v0

--- a/solution.py
+++ b/solution.py
@@ -49,7 +49,8 @@
     width = queries.shape[1]
     scaling = 1.0 / math.sqrt(width)
     cand_block = lax.all_gather(candidates, "pb", axis=0, tiled=True)
-    query_block = lax.all_gather(queries, "col", axis=0, tiled=True)
+    outgoing = jnp.stack([queries] * lax.axis_size("col"))
+    query_block = jnp.concatenate(lax.all_to_all(outgoing, "col", 0, 0), axis=0)
     scores = jnp.dot(query_block, cand_block.T, preferred_element_type=jnp.float32) * scaling
     members = [grades == bucket for bucket in range(GRADES)]
     totals_local = jnp.sum(scores, axis=1)

time: 428 us -> 442 us (1.033)
  blocking collectives: 86.4 us -> 101 us
  waiting for transfers between devices: 231 us -> 217 us
  starting transfers between devices: 0.16 us -> 7.59 us
    all_gather x1 -> x0, waiting for transfers between devices: 52.6 us -> none  [local(): query_block = lax.all_gather(queries, 'col', axis=0, tiled=True)]
    all_to_all x0 -> x1, waiting for transfers between devices: none -> 40.8 us  [local(): query_block = jnp.concatenate(lax.all_to_all(outgoing, 'col', 0, 0), axis=0)]
    all_gather x4, blocking collectives: 86.4 us -> 101 us  [combined_all(): everything = jax.tree.map(lambda part: lax.all_gather(part, axis), x)]
    all_to_all x0 -> x1, starting transfers between devices: none -> 7.46 us  [local(): query_block = jnp.concatenate(lax.all_to_all(outgoing, 'col', 0, 0), axis=0)]
    unnamed x20 -> x18, local copies, waits for them, and re-layouts: 14 us -> 14 us
where the time goes in v1:
time: 442 us; the launch traced here: 441 us
  waiting for transfers between devices  217 us (49%)
  blocking collectives  101 us (23%)
  other arithmetic  44.7 us (10%)
  matrix products  36.9 us (8%)
  local copies, waits for them, and re-layouts  19.4 us (4%)
  between operations  13.9 us (3%)
  starting transfers between devices  7.59 us (2%)
    reduce_scatter x1, waiting for transfers between devices, local(): lax.psum_scatter(jnp.dot(slopes, cand_block, preferred_element_type=jnp.f...  105 us
    all_gather x4, blocking collectives, combined_all(): everything = jax.tree.map(lambda part: lax.all_gather(part, axis), x)  101 us
    reduce_scatter x1, waiting for transfers between devices, local(): lax.psum_scatter(lax.dot_general(slopes, query_block, (((0,), (0,)), ((),...  43.7 us
    all_to_all x1, waiting for transfers between devices, local(): query_block = jnp.concatenate(lax.all_to_all(outgoing, 'col', 0, 0), axis=0)  40.8 us
    all_gather x1, waiting for transfers between devices, local(): cand_block = lax.all_gather(candidates, 'pb', axis=0, tiled=True)  26.8 us
    dot_general x1, matrix products, local(): jnp.dot(query_block, cand_block.T, preferred_element_type=jnp.float32)  19.5 us
    reduce_sum x1, other arithmetic, masses_from(): jnp.sum(jnp.where(members[bucket], expo, 0.0), axis=1)  16.7 us
    add x15, other arithmetic, combine(): former[1] * jnp.exp(former[0] - merged)  14.2 us
  transfers between devices with their start and end apart: 4, of which 4 were waited for; matrix products, arithmetic and copies ran while one was open for 5% of the time, Pallas kernels for 0%

profile of v1, /device:TPU:0, one launch (start us, length us, event | category | flops | bytes accessed | tf_op | source)
XLA Modules:
  0.0 440.8 jit_solution(4253275862876253926)
XLA Ops:
  7.2 3.4 stack.40
  10.6 7.5 %all-to-all-start = ((bf16[16,128,1024]{2,1,0:T(8,128)(2,1)}), bf16[16,128,1024]{2,1,0:T(8,128)(2,1)}, u32[]{:S(2)}, u32[]{:S(2)}) async-start(bf16[16,128,1024]{2,1,0:T(8,128)(2,1)} %stack.40), calls=%async_computation | async-start | bytes 8388608 | tf_op jit(solution)/shard_map/all_to_all | solution.py:53
  18.0 0.0 all-gather.9.cloned.1.call-start
  18.1 0.7 all-gather.9.cloned.1.call-update
  18.8 0.0 reduce-scatter.5.cloned.1.call-start
  18.8 9.1 %copy.14 = s32[2048,1024]{0,1:T(8,128)} copy(s32[2048,1024]{1,0:T(8,128)} %param.8) | data formatting | bytes 16777216 | tf_op args[2]
  28.0 26.8 %all-gather.9.cloned.1.call-done = bf16[1024,1024]{1,0:T(8,128)(2,1)} async-done(((bf16[512,1024]{1,0:T(8,128)(2,1)}), bf16[1024,1024]{1,0:T(8,128)(2,1)}) %all-gather.9.cloned.1.call-update) | async-done | bytes 2097168 | tf_op jit(solution)/shard_map/all_gather | solution.py:51
  54.8 40.8 %all-to-all-done = bf16[16,128,1024]{2,1,0:T(8,128)(2,1)} async-done(((bf16[16,128,1024]{2,1,0:T(8,128)(2,1)}), bf16[16,128,1024]{2,1,0:T(8,128)(2,1)}, u32[]{:S(2)}, u32[]{:S(2)}) %all-to-all-start) | async-done | bytes 4194336 | tf_op jit(solution)/shard_map/all_to_all | solution.py:53
  95.6 19.5 %multiply_reduce_fusion = (f32[2048]{0:T(1024)S(1)}, f32[2048]{0:T(1024)S(1)}, f32[2048]{0:T(1024)S(1)}, f32[2048]{0:T(1024)S(1)}, f32[2048]{0:T(1024)S(1)}, /*i...) fusion(s32[2048,1024]{0,1:T(8,128)} %copy.14, ...), kind=kOutput, calls=%fused_computation.24 | convolution fusion | flops 4334798848 | bytes 33611776 | tf_op jit(solution)/shard_map/dot_general | solution.py:54
  115.1 0.0 copy-start.3
  115.1 0.0 copy-start.4
  115.1 0.0 copy-start.5
  115.1 0.0 copy-start.6
  115.2 35.7 %all-gather.3 = f32[32768]{0:T(1024)S(1)} all-gather(f32[2048]{0:T(1024)S(1)} %get-tuple-element.236), channel_id=5, replica_groups=mesh['pb'=2,'col'=16] {'col'}, dimensions={0}, use_global_device_ids=true | all-gather | bytes 139264 | tf_op jit(solution)/shard_map/all_gather | solution.py:12
  150.9 16.7 %select_reduce_fusion = (f32[2048]{0:T(1024)S(1)}, f32[2048]{0:T(1024)S(1)}, f32[2048]{0:T(1024)S(1)}, f32[2048]{0:T(1024)S(1)}, f32[2048]{0:T(1024)}, /*index=5...) fusion(pred[2048,1024]{0,1:T(8,128)(4,1)} %get-tuple-element.282, ...), kind=kLoop, calls=%fused_computation.13 | loop fusion | flops 52410368 | bytes 27377664 | tf_op jit(solution)/shard_map/reduce_sum | solution.py:70
  167.5 0.0 copy-done.3
  167.6 0.0 copy-done.4
  167.6 0.0 copy-done.5
  167.6 0.0 copy-done.6
  167.6 0.1 stack.99
  167.6 20.5 %all-gather.6 = f32[16,5,2048]{2,1,0:T(8,128)S(1)} all-gather(f32[1,5,2048]{2,1,0:T(8,128)S(1)} %bitcast.72), channel_id=4, replica_groups=mesh['pb'=2,'col'=16] {'col'}, dimensions={0}, use_global_device_ids=true | all-gather | bytes 696320 | tf_op jit(solution)/shard_map/all_gather | solution.py:12
  188.1 0.8 stack.93
  188.9 23.7 %all-gather.5 = f32[16,5,2048]{2,1,0:T(8,128)S(1)} all-gather(f32[1,5,2048]{2,1,0:T(8,128)S(1)} %bitcast.73), channel_id=3, replica_groups=mesh['pb'=2,'col'=16] {'col'}, dimensions={0}, use_global_device_ids=true | all-gather | bytes 696320 | tf_op jit(solution)/shard_map/all_gather | solution.py:12
  212.6 1.1 copy-done.1
  213.7 0.8 stack.87
  214.5 20.8 %all-gather.4 = f32[16,5,2048]{2,1,0:T(8,128)S(1)} all-gather(f32[1,5,2048]{2,1,0:T(8,128)S(1)} %bitcast.71), channel_id=2, replica_groups=mesh['pb'=2,'col'=16] {'col'}, dimensions={0}, use_global_device_ids=true | all-gather | bytes 696320 | tf_op jit(solution)/shard_map/all_gather | solution.py:12
  235.3 1.0 copy-done.2
  236.3 15.0 %while.21 = (s32[]{:T(128)}, f32[5,2048]{1,0:T(8,128)S(1)}, f32[5,2048]{1,0:T(8,128)S(1)}, f32[5,2048]{1,0:T(8,128)S(1)}, f32[2048]{0:T(1024)S(1)}, /*index=5*/f...) while((s32[]{:T(128)}, f32[5,2048]{1,0:T(8,128)S(1)}, ...), condition=%wide.region_17.18_spmd, body=%wide.region_16.17_spmd.sunk | while | flops 73733 | bytes 409767 | solution.py:18
  236.3 0.9 fusion.46
  237.3 0.9 fusion.46
  238.3 0.9 fusion.46
  239.3 0.9 fusion.46
  240.3 0.9 fusion.46
  241.3 0.9 fusion.46
  242.3 0.9 fusion.46
  243.3 0.9 fusion.46
  244.3 0.9 fusion.46
  245.3 0.9 fusion.46
  246.3 0.9 fusion.46
  247.3 0.9 fusion.46
  248.3 0.9 fusion.46
  249.3 0.9 fusion.46
  250.3 0.9 fusion.46
  251.3 0.2 exponential_multiply_fusion.1
  251.5 0.2 multiply_add_fusion.2
  251.7 0.1 multiply_add_fusion.3
  251.8 0.1 multiply_add_fusion.4
  251.9 0.2 multiply_add_fusion.5
  252.1 0.1 stack.100
  252.2 8.6 %multiply_convert_fusion = bf16[2048,1024]{0,1:T(8,128)(2,1)S(1)} fusion(f32[2048,1024]{0,1:T(8,128)} %get-tuple-element.280, pred[2048,1024]{0,1:T(8,128)(4,1)} %get-tuple-element.282, pred[2048,1024]{0,1:T(8,128)(4,1)} %get-tuple-element.283, pred[2048,1024]{0,1:T(8,128)(4,1)} %get-tuple-element.284, pred[2048,1024]{0,1:T(8,128)(4,1)} %get-tuple-element.285, ...), kind=kLoop, calls=%fused_computation.7 | loop fusion | flops 18874368 | bytes 23117824 | tf_op jit(solution)/shard_map/convert_element_type | solution.py:90
  260.8 0.0 copy-start
  260.8 1.9 copy-done
  262.8 8.4 %convolution_multiply_fusion.1 = f32[1024,1024]{1,0:T(8,128)} fusion(bf16[2048,1024]{0,1:T(8,128)(2,1)S(1)} %multiply_convert_fusion, bf16[2048,1024]{1,0:T(8,128)(2,1)} %bitcast.4), kind=kOutput, calls=%fused_computation.31 | convolution fusion | flops 4296015872 | bytes 12582912 | tf_op jit(solution)/shard_map/dot_general | solution.py:100
  271.1 0.0 reduce-scatter.5.cloned.1.call-update
  271.2 0.0 reduce-scatter.3.cloned.1.call-start
  271.2 0.0 copy-done.7
  271.2 9.0 %convolution_multiply_fusion = f32[2048,1024]{0,1:T(8,128)} fusion(bf16[2048,1024]{0,1:T(8,128)(2,1)} %copy-done, bf16[1024,1024]{1,0:T(8,128)(2,1)S(1)} %copy-done.7), kind=kOutput, calls=%fused_computation.25 | convolution fusion | flops 4297064448 | bytes 14680064 | tf_op jit(solution)/shard_map/dot_general | solution.py:94
  280.2 0.0 reduce-scatter.3.cloned.1.call-update
  280.3 0.7 fusion.9
  280.9 43.7 %reduce-scatter.5.cloned.1.call-done = f32[512,1024]{1,0:T(8,128)} async-done(((f32[1024,1024]{1,0:T(8,128)}), f32[512,1024]{1,0:T(8,128)}) %reduce-scatter.5.cloned.1.call-update) | async-done | bytes 2097168 | tf_op jit(solution)/shard_map/reduce_scatter | solution.py:99
  324.6 2.7 convert_element_type.31
  327.3 105.0 %reduce-scatter.3.cloned.1.call-done = f32[128,1024]{0,1:T(8,128)} async-done(((f32[2048,1024]{0,1:T(8,128)}), f32[128,1024]{0,1:T(8,128)}) %reduce-scatter.3.cloned.1.call-update) | async-done | bytes 524304 | tf_op jit(solution)/shard_map/reduce_scatter | solution.py:93
  432.3 1.1 convert_element_type.30
  433.4 0.8 copy.20
  (40 shorter events, 0.4 us)
Async XLA Ops:
  10.6 85.0 %all-to-all-start = ((bf16[16,128,1024]{2,1,0:T(8,128)(2,1)}), bf16[16,128,1024]{2,1,0:T(8,128)(2,1)}, u32[]{:S(2)}, u32[]{:S(2)}) async-start(bf16[16,128,1024]{2,1,0:T(8,128)(2,1)} %stack.40), calls=%async_computation | async-start | bytes 8388608 | tf_op jit(solution)/shard_map/all_to_all | solution.py:53
  18.0 36.7 %all-gather.9.cloned.1.call-start = ((), (), s32[]{:S(2)}) async-start(), calls=%async_computation.3 | async-start | bytes 3145728 | tf_op jit(solution)/shard_map/all_gather | solution.py:51
  18.8 305.8 %reduce-scatter.5.cloned.1.call-start = ((), (), s32[]{:S(2)}) async-start(), calls=%async_computation.5 | async-start | bytes 6291456 | tf_op jit(solution)/shard_map/reduce_scatter | solution.py:99
  115.1 52.4 %copy-start.3 = (f32[2048]{0:T(1024)}, f32[2048]{0:T(1024)S(1)}, u32[]{:S(2)}) copy-start(f32[2048]{0:T(1024)S(1)} %get-tuple-element.238) | copy-start | bytes 24580
  115.1 52.4 %copy-start.4 = (f32[2048]{0:T(1024)}, f32[2048]{0:T(1024)S(1)}, u32[]{:S(2)}) copy-start(f32[2048]{0:T(1024)S(1)} %get-tuple-element.239) | copy-start | bytes 24580
  115.1 52.4 %copy-start.5 = (f32[2048]{0:T(1024)}, f32[2048]{0:T(1024)S(1)}, u32[]{:S(2)}) copy-start(f32[2048]{0:T(1024)S(1)} %get-tuple-element.240) | copy-start | bytes 24580
  115.1 52.4 %copy-start.6 = (f32[2048]{0:T(1024)}, f32[2048]{0:T(1024)S(1)}, u32[]{:S(2)}) copy-start(f32[2048]{0:T(1024)S(1)} %get-tuple-element.241) | copy-start | bytes 24580
  212.6 1.1 copy-start.1
  235.3 1.0 copy-start.2
  260.8 2.0 copy-start
  262.8 8.5 %copy-start.7 = (bf16[1024,1024]{1,0:T(8,128)(2,1)S(1)}, bf16[1024,1024]{1,0:T(8,128)(2,1)}, u32[]{:S(2)}) copy-start(bf16[1024,1024]{1,0:T(8,128)(2,1)} %all-gather.9.cloned.1.call-done) | copy-start | bytes 6291460
  271.2 161.1 %reduce-scatter.3.cloned.1.call-start = ((), (), s32[]{:S(2)}) async-start(), calls=%async_computation.4 | async-start | bytes 8912896 | tf_op jit(solution)/shard_map/reduce_scatter | solution.py:93
Sparse Core Ops, SparseCore 0:
  20.4 34.3 all-gather.8
  271.3 53.2 reduce-scatter.4
  328.7 103.5 reduce-scatter.2
